TPU v7x, 64 devices: a 2x2x8 block of a 4x4x8 slice. The times are simulated.
64 devices in a mesh: dp: 8 (over x, y, core), sp: 8 (over z).
Axes of the slice: x: 2, y: 2, z: 8, core: 2. Of those that a mesh axis runs over, the one named last changes fastest.
The devices are a block of a 4x4x8 slice.
Arguments:
- q: bfloat16 [256, 32, 64], P('dp'), parts along dimension 0
- k: bfloat16 [256, 8192, 8, 64], P('dp', 'sp'), parts along dimension 0
- v: bfloat16 [256, 8192, 8, 64], P('dp', 'sp'), parts along dimension 0
Outputs:
- q: bfloat16 [256, 32, 64], P('dp'), parts along dimension 0
There are 8 independent parts. A program takes and returns all parts, laid end to end along the dimension named above; each array names one.
All inputs are finite; a program needn't handle non-finite values.
Results may differ from a plain program's by a relative error of at most 0.012.
Values are sent between devices in bfloat16 or wider.
A program may use at most 768 MiB of HBM per device.

v0:
```python
import jax
import jax.numpy as jnp
from jax import lax
from jax.sharding import PartitionSpec as P


def einsum(form, a, b):
    return jnp.einsum(form, a.astype(jnp.float32), b.astype(jnp.float32))


def part_of(q, k, v):
    grouped = q.reshape(q.shape[0], k.shape[2], -1, q.shape[2])
    scores = einsum("bgsd,bugd->bgsu", grouped, k) * q.shape[2] ** -0.5
    high = jnp.max(scores, -1, keepdims=True)
    weights = jnp.exp(scores - high)
    seen = einsum("bgsu,bugd->bgsd", weights.astype(jnp.bfloat16), v)
    return jnp.concatenate([seen, jnp.sum(weights, -1, keepdims=True), high], -1)


def together(parts):
    seen, total, high = parts[..., :-2], parts[..., -2:-1], parts[..., -1:]
    scale = jnp.exp(high - jnp.max(high, 0))
    return (jnp.sum(seen * scale, 0) / jnp.sum(total * scale, 0)).astype(jnp.bfloat16)


def solution(mesh):
    def step(q, k, v):
        return together(lax.all_gather(part_of(q, k, v), "sp")).reshape(q.shape)

    return jax.shard_map(
        step,
        mesh=mesh,
        in_specs=(P("dp", None, None), P("dp", "sp", None, None), P("dp", "sp", None, None)),
        out_specs=P("dp", None, None),
        check_vma=False,
    )
```

profile of v0, /device:TPU:21, one launch (start us, length us, event | category | flops | bytes accessed | tf_op | source)
XLA Modules:
  0.0 125.1 jit_solution(15638022340023534964)
XLA Ops:
  6.5 0.0 copy-start
  6.6 0.0 all-gather.3.cloned.1.call-start
  6.6 0.9 copy-done
  7.5 12.9 %multiply_reduce_fusion = (f32[32,8,4]{2,1,0:T(8,128)S(1)}, f32[32,8,4,1024]{3,2,1,0:T(4,128)S(1)}) fusion(bf16[32,8,4,64]{3,2,1,0:T(4,128)(2,1)S(1)} %bitcast.14, bf16[32,1024,8,64]{1,3,2,0:T(8,128)(2,1)} %param.4), kind=kOutput, calls=%fused_computation.3 | convolution fusion | flops 136313856 | bytes 37883904 | tf_op jit(solution)/shard_map/bgsd,bugd->bgsu/dot_general | solution.py:8
  20.4 2.0 %fusion.1 = f32[32,8,4]{2,1,0:T(8,128)S(1)} fusion(f32[32,8,4,1024]{3,2,1,0:T(4,128)S(1)} %get-tuple-element.11, f32[32,8,4]{2,1,0:T(8,128)S(1)} %get-tuple-element.10), kind=kLoop, calls=%fused_computation.4 | loop fusion | flops 3144704 | bytes 4202496 | tf_op jit(solution)/shard_map/reduce_sum | solution.py:17
  22.5 14.2 %fusion.3 = f32[32,8,4,64]{3,2,1,0:T(4,128)S(1)} fusion(bf16[32,1024,8,64]{1,3,2,0:T(8,128)(2,1)} %param.5, f32[32,8,4,1024]{3,2,1,0:T(4,128)S(1)} %get-tuple-element.11, f32[32,8,4]{2,1,0:T(8,128)S(1)} %get-tuple-element.10), kind=kOutput, calls=%fused_computation.6 | convolution fusion | flops 137363456 | bytes 38014976 | tf_op jit(solution)/shard_map/bgsu,bugd->bgsd/dot_general | solution.py:8
  36.6 1.7 %copy.51 = f32[32,8,4,1]{3,2,1,0:T(4,128)S(1)} copy(f32[32,8,4,1]{2,1,0,3:T(8,128)S(1)} %bitcast.18) | data formatting | bytes 8192 | tf_op jit(solution)/shard_map/broadcast_in_dim | solution.py:17
  38.3 1.7 %copy.52 = f32[32,8,4,1]{3,2,1,0:T(4,128)S(1)} copy(f32[32,8,4,1]{2,1,0,3:T(8,128)S(1)} %bitcast.17) | data formatting | bytes 8192 | tf_op jit(solution)/shard_map/broadcast_in_dim | solution.py:14
  40.0 0.6 pad_maximum_fusion
  40.6 0.8 copy.53
  41.4 0.1 all-gather.3.cloned.1.call-update
  41.5 55.9 %all-gather.3.cloned.1.call-done = f32[256,8,4,66]{3,1,2,0:T(8,128)} async-done(((f32[32,8,4,66]{3,1,2,0:T(8,128)}), f32[256,8,4,66]{3,1,2,0:T(8,128)}) %all-gather.3.cloned.1.call-update) | async-done | bytes 2162704 | tf_op jit(solution)/shard_map/all_gather | solution.py:28
  97.4 9.0 %fusion.10 = (f32[8,32,8,4,1]{4,2,3,1,0:T(8,128)}, f32[32,8,4]{1,2,0:T(4,128)S(1)}, f32[8,32,8,4,1]{4,2,3,1,0:T(8,128)}) fusion(f32[8,32,8,4,66]{4,2,3,1,0:T(8,128)} %bitcast.15), kind=kLoop, calls=%fused_computation.17 | loop fusion | flops 7168 | bytes 135168 | tf_op jit(solution)/shard_map/slice | solution.py:21
  106.4 3.6 %copy.65 = f32[8,32,8,4,1]{1,2,4,3,0:T(8,128)S(1)} copy(f32[8,32,8,4,1]{4,2,3,1,0:T(8,128)} %get-tuple-element.5) | data formatting | bytes 65536
  110.0 0.1 copy.66
  110.1 3.6 %copy.64 = f32[8,32,8,4,1]{1,2,4,3,0:T(8,128)S(1)} copy(f32[8,32,8,4,1]{4,2,3,1,0:T(8,128)} %get-tuple-element.7) | data formatting | bytes 65536
  113.7 0.0 copy-start.1
  113.7 0.2 copy.55
  114.0 2.9 %fusion = f32[32,8,4,64]{3,1,2,0:T(8,128)S(1)} fusion(f32[8,32,8,4,66]{4,2,3,1,0:T(8,128)} %bitcast.16, f32[8,32,8,4]{2,3,1,0:T(4,128)S(1)} %copy.55), kind=kLoop, calls=%fused_computation.1 | loop fusion | flops 983040 | bytes 2392064 | tf_op jit(solution)/shard_map/reduce_sum | solution.py:23
  116.9 0.3 copy.56
  117.2 0.2 fusion.7
  117.4 0.8 copy.59
  118.2 0.0 copy-done.1
  (2 shorter events, 0.0 us)
Async XLA Ops:
  6.5 1.0 copy-start
  6.6 90.8 %all-gather.3.cloned.1.call-start = ((), (), s32[]{:S(2)}) async-start(), calls=%async_computation | async-start | bytes 4718592 | tf_op jit(solution)/shard_map/all_gather | solution.py:28
  113.7 4.6 %copy-start.1 = (bf16[32,32,64]{2,1,0:T(8,128)(2,1)S(1)}, bf16[32,32,64]{2,1,0:T(8,128)(2,1)}, u32[]{:S(2)}) copy-start(bf16[32,32,64]{2,1,0:T(8,128)(2,1)} %param.3) | copy-start | bytes 393220
Sparse Core Ops, SparseCore 0:
  41.6 55.7 all-gather.2
where the time goes:
time: 125 us
  waiting for transfers between devices  56 us (45%)
  matrix products  27.1 us (22%)
  other arithmetic  14.8 us (12%)
  local copies, waits for them, and re-layouts  13.8 us (11%)
  between operations  13.5 us (11%)
    all_gather x1, waiting for transfers between devices, step(): return together(lax.all_gather(part_of(q, k, v), 'sp')).reshape(q.shape)  55.9 us
    dot_general x2, matrix products, einsum(): return jnp.einsum(form, a.astype(jnp.float32), b.astype(jnp.float32))  27.1 us
    slice x1, other arithmetic, together(): seen, total, high = (parts[..., :-2], parts[..., -2:-1], parts[..., -1:])  8.99 us
    unnamed x7, local copies, waits for them, and re-layouts  8.25 us
    reduce_sum x1, other arithmetic, together(): jnp.sum(seen * scale, 0) / jnp.sum(total * scale, 0)  2.89 us
  transfers between devices with their start and end apart: 1, of which 1 were waited for; matrix products, arithmetic and copies ran while one was open for 0% of the time, Pallas kernels for 0%

commit v1 on v0

v1 whole, which is shorter than its diff:
```python
import functools
import math

import jax
import jax.numpy as jnp
from jax import lax
from jax.experimental import pallas as pl
from jax.experimental.pallas import tpu as pltpu
from jax.sharding import PartitionSpec as P

SLOTS = 6
STEP = 2


def kernel(
    devices, rounds, q_hbm, k_hbm, v_hbm, out_ref,
    q_ref, keys, values, scores, part, stat, parts, stats, done,
    q_sem, k_sem, v_sem, send_part, send_stat, recv_part, recv_stat, send_done, recv_done,
):
    sequences, heads, depth = q_hbm.shape
    shared = rounds * devices
    factor = depth**-0.5 * math.log2(math.e)
    me = lax.axis_index("sp")
    order = sorted(range(1, devices), key=lambda d: -min(d, devices - d))

    def device(i):
        return {"sp": i}

    def fetch(hbm, buffer, sem, s):
        slot = lax.rem(s, SLOTS)
        return pltpu.make_async_copy(hbm.at[s], buffer.at[slot], sem.at[slot])

    def fetch_k(s):
        return fetch(k_hbm, keys, k_sem, s)

    def fetch_v(s):
        return fetch(v_hbm, values, v_sem, s)

    fetch_q = pltpu.make_async_copy(q_hbm, q_ref, q_sem)
    fetch_q.start()
    for s in range(SLOTS):
        fetch_k(s).start()
        fetch_v(s).start()
    barrier = pltpu.get_barrier_semaphore()
    for d in order:
        pl.semaphore_signal(barrier, inc=1, device_id=device(lax.rem(me + d, devices)), device_id_type=pl.DeviceIdType.MESH)

    half = heads // 2
    own = lax.broadcasted_iota(jnp.int32, (half, 4 * depth), 0) // 4 == lax.broadcasted_iota(jnp.int32, (half, 4 * depth), 1) // depth
    lane = lax.broadcasted_iota(jnp.int32, (8, 128), 1)
    row = lax.broadcasted_iota(jnp.int32, (8, 128), 0)
    left, upper = lane < 64, row < 4
    lane32 = lax.broadcasted_iota(jnp.int32, (32, 128), 1)
    row32 = lax.broadcasted_iota(jnp.int32, (32, 128), 0)
    place = lax.rem(row32 // 4, 2) * 16 + row32 // 8 * 4 + lax.rem(row32, 4)
    lane16 = lax.broadcasted_iota(jnp.int32, (16, 128), 1)
    row16 = lax.broadcasted_iota(jnp.int32, (16, 128), 0)

    def score(s, slot):
        q = q_ref[s]
        q = jnp.concatenate([q, q], 1)
        q = jnp.concatenate([q, q], 1)
        for g in range(2):
            rows = pl.ds(half * g, half)
            mine = jnp.where(own, q[half * g : half * (g + 1)].astype(jnp.float32), 0.0).astype(jnp.bfloat16)
            block = keys[lax.rem(s, SLOTS), pl.ds(4 * depth * g, 4 * depth), :]
            scores[slot, rows, :] = jnp.dot(mine, block, preferred_element_type=jnp.float32)

    def attend(s, slot):
        seen, highs, totals = [], [], []
        for g in range(2):
            x = scores[slot, pl.ds(half * g, half), :]
            high = jnp.max(x, -1, keepdims=True)
            weights = jnp.exp2((x - high) * factor)
            highs.append(high)
            totals.append(jnp.sum(weights, -1, keepdims=True))
            block = values[lax.rem(s, SLOTS), pl.ds(4 * depth * g, 4 * depth), :]
            o = lax.dot_general(weights.astype(jnp.bfloat16), block, (((1,), (1,)), ((), ())), preferred_element_type=jnp.float32)
            a, b = o[:8, :128], o[8:, 128:]
            a = jnp.where(left, a, pltpu.roll(a, 4, 0))
            b = jnp.where(left, pltpu.roll(b, 4, 0), b)
            seen.append(jnp.where(upper, a, b))
        part[s] = jnp.concatenate(seen, 0).astype(jnp.bfloat16)
        both = jnp.where(lane32 == place, jnp.concatenate(highs, 0), 0.0) + jnp.where(lane32 == place + 32, jnp.concatenate(totals, 0), 0.0)
        stat[s] = jnp.sum(both, 0, keepdims=True)

    def send(s, slot, to):
        pltpu.make_async_remote_copy(part.at[s], parts.at[slot, me], send_part.at[slot], recv_part.at[slot], device(to), pl.DeviceIdType.MESH).start()
        pltpu.make_async_remote_copy(stat.at[s], stats.at[slot, me], send_stat.at[slot], recv_stat.at[slot], device(to), pl.DeviceIdType.MESH).start()

    def leave(s):
        @pl.when(s < shared)
        def _():
            owner = lax.rem(s, devices)

            @pl.when(owner != me)
            def _():
                send(s, s // devices, owner)

        @pl.when(s >= shared)
        def _():
            for d in order:
                send(s, rounds + s - shared, lax.rem(me + d, devices))

    def others(ref, slot, sends, recvs):
        some = ref.at[slot, pl.ds(0, devices - 1)]
        return pltpu.make_async_remote_copy(some, some, sends.at[slot], recvs.at[slot], device(lax.rem(me + 1, devices)), pl.DeviceIdType.MESH)

    def together(slot, s):
        parts[slot, me] = part[s]
        stats[slot, me] = stat[s]
        others(parts, slot, send_part, recv_part).wait_recv()
        others(stats, slot, send_stat, recv_stat).wait_recv()
        st = stats[slot].reshape(devices, 128)
        scale = jnp.exp2((st - jnp.max(st, 0, keepdims=True)) * factor)
        total = jnp.sum(scale * pltpu.roll(st, 96, 1), 0, keepdims=True)
        scale = scale / total
        out = jnp.zeros((16, 128), jnp.float32)
        for j in range(devices):
            one = scale[j : j + 1]
            even = jnp.sum(jnp.where(lane16 == row16, one, 0.0), 1, keepdims=True)
            odd = jnp.sum(jnp.where(lane16 == row16 + 16, one, 0.0), 1, keepdims=True)
            out = out + parts[slot, j].astype(jnp.float32) * jnp.where(lane16 < 64, even, odd)
        return out

    def write(s, x):
        rows = []
        for j in range(2):
            v = x[8 * j : 8 * (j + 1)]
            w = pltpu.roll(v, 64, 1)
            rows += [jnp.where(upper, v, pltpu.roll(w, 4, 0)), jnp.where(upper, pltpu.roll(v, 4, 0), w)]
        out_ref[s] = jnp.concatenate(rows, 0).astype(jnp.bfloat16)

    def share(r):
        s = r * devices + me
        done[r, me] = together(r, s).astype(jnp.bfloat16)
        for d in order:
            to = lax.rem(me + d, devices)
            pltpu.make_async_remote_copy(done.at[r, me], done.at[r, me], send_done.at[r], recv_done.at[r], device(to), pl.DeviceIdType.MESH).start()

    fetch_q.wait()
    for u in range(STEP):
        fetch_k(u).wait()
        score(u, u)
    for u in range(STEP):
        fetch_k(u + SLOTS).start()

    steps = sequences // STEP
    turn = devices // STEP

    def body(i, _):
        s = i * STEP
        now = lax.rem(i, 2) * STEP

        @pl.when(i == 1)
        def _():
            pl.semaphore_wait(barrier, devices - 1)

        @pl.when(i > 0)
        def _():
            for u in range(STEP):
                leave(s - STEP + u)

        for r in range(rounds):
            @pl.when(i == turn * r + 2 * turn - 1)
            def _():
                share(r)

        @pl.when(i < steps - 1)
        def _():
            for u in range(STEP):
                fetch_k(s + STEP + u).wait()

        for u in range(STEP):
            fetch_v(s + u).wait()
        for u in range(STEP):
            score(jnp.minimum(s + STEP + u, sequences - 1), STEP - now + u)
        for u in range(STEP):
            attend(s + u, now + u)
        for u in range(STEP):
            t = s + STEP + SLOTS + u

            @pl.when(t < sequences)
            def _():
                fetch_k(t).start()

            @pl.when(t - STEP < sequences)
            def _():
                fetch_v(t - STEP).start()

        return 0

    lax.fori_loop(0, steps, body, 0)
    for u in range(STEP):
        leave(sequences - STEP + u)

    for r in range(rounds):
        others(done, r, send_done, recv_done).wait_recv()

        def emit(j, _):
            write(r * devices + j, done[r, j].astype(jnp.float32))
            return 0

        lax.fori_loop(0, devices, emit, 0)

    def finish(j, _):
        write(shared + j, together(rounds + j, shared + j))
        return 0

    lax.fori_loop(0, sequences - shared, finish, 0)

    for r in range(rounds):
        others(done, r, send_done, recv_done).wait_send()

    def drain(slot, _):
        others(parts, slot, send_part, recv_part).wait_send()
        others(stats, slot, send_stat, recv_stat).wait_send()
        return 0

    lax.fori_loop(0, rounds + sequences - shared, drain, 0)


def solution(mesh):
    devices = mesh.shape["sp"]

    def step(q, k, v):
        n, heads, depth = q.shape
        tokens, groups = k.shape[1:3]
        rounds = n // devices - 1
        slots = rounds + devices
        k, v = (x.transpose(0, 2, 3, 1).reshape(n, groups * depth, tokens) for x in (k, v))
        out = pl.pallas_call(
            functools.partial(kernel, devices, rounds),
            out_shape=jax.ShapeDtypeStruct((n, heads, 128), jnp.bfloat16),
            in_specs=[pl.BlockSpec(memory_space=pl.ANY)] * 3,
            out_specs=pl.BlockSpec(memory_space=pltpu.VMEM),
            scratch_shapes=[
                pltpu.VMEM((n, heads, depth), jnp.bfloat16),
                pltpu.VMEM((SLOTS, groups * depth, tokens), jnp.bfloat16),
                pltpu.VMEM((SLOTS, groups * depth, tokens), jnp.bfloat16),
                pltpu.VMEM((2 * STEP, heads, tokens), jnp.float32),
                pltpu.VMEM((n, 16, 128), jnp.bfloat16),
                pltpu.VMEM((n, 1, 128), jnp.float32),
                pltpu.VMEM((slots, devices, 16, 128), jnp.bfloat16),
                pltpu.VMEM((slots, devices, 1, 128), jnp.float32),
                pltpu.VMEM((rounds, devices, 16, 128), jnp.bfloat16),
                pltpu.SemaphoreType.DMA,
                pltpu.SemaphoreType.DMA((SLOTS,)),
                pltpu.SemaphoreType.DMA((SLOTS,)),
                pltpu.SemaphoreType.DMA((slots,)),
                pltpu.SemaphoreType.DMA((slots,)),
                pltpu.SemaphoreType.DMA((slots,)),
                pltpu.SemaphoreType.DMA((slots,)),
                pltpu.SemaphoreType.DMA((rounds,)),
                pltpu.SemaphoreType.DMA((rounds,)),
            ],
            compiler_params=pltpu.CompilerParams(collective_id=0, has_side_effects=True, vmem_limit_bytes=60 * 2**20),
        )(q, k, v)
        return out[:, :, :depth]

    return jax.shard_map(
        step,
        mesh=mesh,
        in_specs=(P("dp", None, None), P("dp", "sp", None, None), P("dp", "sp", None, None)),
        out_specs=P("dp", None, None),
        check_vma=False,
    )
```

time: 125 us -> 42.2 us (0.34)
  waiting for transfers between devices: 56 us -> 0 us
  Pallas kernels: 0 us -> 39.7 us
  matrix products: 27.1 us -> 0 us
  other arithmetic: 14.8 us -> 0 us
  between operations: 13.5 us -> 0.01 us
  local copies, waits for them, and re-layouts: 13.8 us -> 1.67 us
    all_gather x1 -> x0, waiting for transfers between devices: 55.9 us -> none  [step(): return together(lax.all_gather(part_of(q, k, v), 'sp')).reshape(q.shape)]
    pallas_call x0 -> x1, Pallas kernels: none -> 39.7 us  [step(): pl.pallas_call(functools.partial(kernel, devices, rounds), out_shape=jax....]
    dot_general x2 -> x0, matrix products: 27.1 us -> none  [einsum(): return jnp.einsum(form, a.astype(jnp.float32), b.astype(jnp.float32))]
    slice x1 -> x0, other arithmetic: 8.99 us -> none  [together(): seen, total, high = (parts[..., :-2], parts[..., -2:-1], parts[..., -1:])]
    unnamed x7 -> x1, local copies, waits for them, and re-layouts: 8.25 us -> 1.67 us
    reduce_sum x3 -> x0, other arithmetic: 4.97 us -> none  [the longest x1 2.89 us: together(): jnp.sum(seen * scale, 0) / jnp.sum(total * scale, 0)]
    broadcast_in_dim x2 -> x0, local copies, waits for them, and re-layouts: 3.33 us -> none  [the longest x1 1.66 us: part_of(): jnp.sum(weights, -1, keepdims=True)]
  transfers between devices with their start and end apart: 1 -> 0, of which waited for: 1 -> 0; matrix products, arithmetic and copies ran while one was open for 0% -> 0% of each run, Pallas kernels for 0% -> 0%
where the time goes in v1:
time: 42.2 us; the launch traced here: 41.4 us
  Pallas kernels  39.7 us (94%)
  local copies, waits for them, and re-layouts  1.67 us (4%)
    pallas_call x1, Pallas kernels, step(): pl.pallas_call(functools.partial(kernel, devices, rounds), out_shape=jax....  39.7 us
    unnamed x1, local copies, waits for them, and re-layouts  1.67 us

profile of v1, /device:TPU:21, one launch (start us, length us, event | category | flops | bytes accessed | tf_op | source)
XLA Modules:
  0.0 41.4 jit_solution(1258261064216510645)
XLA Ops:
  0.0 39.7 %shard_map.37 = bf16[32,32,128]{2,1,0:T(8,128)(2,1)} custom-call(bf16[32,32,64]{2,1,0:T(8,128)(2,1)} %q_hbm.1, bf16[32,512,1024]{2,1,0:T(8,128)(2,1)} %bitcast.7, bf16[32,512,1024]{2,1,0:T(8,128)(2,1)} %bitcast.8), custom_call_target="tpu_custom_call" | custom-call | tf_op jit(solution)/shard_map/pallas_call | solution.py:232
  39.7 1.7 %copy.5 = bf16[32,32,64]{2,1,0:T(8,128)(2,1)} copy(bf16[32,32,64]{2,1,0:T(8,128)(2,1)} %bitcast.9) | data formatting | bytes 262144

commit v2 on v1

v2 whole, which is shorter than its diff:
```python
import functools
import math

import jax
import jax.numpy as jnp
from jax import lax
from jax.experimental import pallas as pl
from jax.experimental.pallas import tpu as pltpu
from jax.sharding import PartitionSpec as P

SLOTS = 6
STEP = 2
DIRECT = 2
GREET = 3


def kernel(
    devices, q_hbm, k_hbm, v_hbm, out_ref,
    q_ref, keys, values, scores, part, stat, owner_parts, owner_stats, parts, stats, done,
    q_sem, k_sem, v_sem, send_part, send_stat, owner_recv_part, owner_recv_stat, recv_part, recv_stat, send_done, recv_done,
):
    sequences, heads, depth = q_hbm.shape
    shared = sequences - DIRECT
    spread = 2 * devices
    front = devices // 2
    near = spread + front
    factor = depth**-0.5 * math.log2(math.e)
    me = lax.axis_index("sp")
    order = sorted(range(1, devices), key=lambda d: -min(d, devices - d))

    def device(i):
        return {"sp": i}

    def fetch(hbm, buffer, sem, s):
        slot = lax.rem(s, SLOTS)
        return pltpu.make_async_copy(hbm.at[s], buffer.at[slot], sem.at[slot])

    def in_pieces(hbm, buffer, sem, s):
        slot = lax.rem(s, SLOTS)
        size = buffer.shape[1] // 4
        for piece in range(4):
            rows = pl.ds(piece * size, size)
            pltpu.make_async_copy(hbm.at[s, rows], buffer.at[slot, rows], sem.at[slot]).start()

    def fetch_k(s):
        return fetch(k_hbm, keys, k_sem, s)

    def fetch_v(s):
        return fetch(v_hbm, values, v_sem, s)

    fetch_q = pltpu.make_async_copy(q_hbm, q_ref, q_sem)
    fetch_q.start()
    for u in range(STEP):
        fetch_k(u).start()
    for u in range(STEP):
        fetch_v(u).start()
    barrier = pltpu.get_barrier_semaphore()
    for d in order:
        pl.semaphore_signal(barrier, inc=1, device_id=device(lax.rem(me + d, devices)), device_id_type=pl.DeviceIdType.MESH)

    half = heads // 2
    own = lax.broadcasted_iota(jnp.int32, (half, 4 * depth), 0) // 4 == lax.broadcasted_iota(jnp.int32, (half, 4 * depth), 1) // depth
    lane = lax.broadcasted_iota(jnp.int32, (8, 128), 1)
    row = lax.broadcasted_iota(jnp.int32, (8, 128), 0)
    left, upper = lane < 64, row < 4
    lane32 = lax.broadcasted_iota(jnp.int32, (32, 128), 1)
    row32 = lax.broadcasted_iota(jnp.int32, (32, 128), 0)
    place = lax.rem(row32 // 4, 2) * 16 + row32 // 8 * 4 + lax.rem(row32, 4)
    lane16 = lax.broadcasted_iota(jnp.int32, (16, 128), 1)
    row16 = lax.broadcasted_iota(jnp.int32, (16, 128), 0)

    def score(s, slot):
        q = q_ref[s]
        q = jnp.concatenate([q, q], 1)
        q = jnp.concatenate([q, q], 1)
        for g in range(2):
            rows = pl.ds(half * g, half)
            mine = jnp.where(own, q[half * g : half * (g + 1)].astype(jnp.float32), 0.0).astype(jnp.bfloat16)
            block = keys[lax.rem(s, SLOTS), pl.ds(4 * depth * g, 4 * depth), :]
            scores[slot, rows, :] = jnp.dot(mine, block, preferred_element_type=jnp.float32)

    def attend(s, slot):
        seen, highs, totals = [], [], []
        for g in range(2):
            x = scores[slot, pl.ds(half * g, half), :]
            high = jnp.max(x, -1, keepdims=True)
            weights = jnp.exp2((x - high) * factor)
            highs.append(high)
            totals.append(jnp.sum(weights, -1, keepdims=True))
            block = values[lax.rem(s, SLOTS), pl.ds(4 * depth * g, 4 * depth), :]
            o = lax.dot_general(weights.astype(jnp.bfloat16), block, (((1,), (1,)), ((), ())), preferred_element_type=jnp.float32)
            a, b = o[:8, :128], o[8:, 128:]
            a = jnp.where(left, a, pltpu.roll(a, 4, 0))
            b = jnp.where(left, pltpu.roll(b, 4, 0), b)
            seen.append(jnp.where(upper, a, b))
        part[s] = jnp.concatenate(seen, 0).astype(jnp.bfloat16)
        both = jnp.where(lane32 == place, jnp.concatenate(highs, 0), 0.0) + jnp.where(lane32 == place + 32, jnp.concatenate(totals, 0), 0.0)
        stat[s] = jnp.sum(both, 0, keepdims=True)

    def owner_of(s):
        late = jnp.maximum(0, front - 1 - (s - near) // STEP)
        return jnp.where(s < spread, lax.rem(s, devices), jnp.where(s < near, s - spread + front, late))

    def first_of(d):
        return near + (front - 1 - d) * STEP

    def slot_of(s):
        return jnp.where(s < spread, s // devices, jnp.where(s < near, 2, 2 + s - first_of(owner_of(s))))

    def remote(src, dst, send, recv, to):
        return pltpu.make_async_remote_copy(src, dst, send, recv, device(to), pl.DeviceIdType.MESH)

    def leave(i):
        for u in range(STEP):
            s = i * STEP + u
            owner = jnp.where(i < spread // STEP, lax.rem(i * STEP, devices) + u, jnp.where(i < near // STEP, s - spread + front, jnp.maximum(0, front - 1 + near // STEP - i)))
            more = jnp.maximum(0, i - (near // STEP + front - 1)) * STEP + u
            slot = jnp.where(i < spread // STEP, i * STEP // devices, jnp.where(i < near // STEP, 2, 2 + more))

            @pl.when(owner != me)
            def _():
                remote(part.at[s], owner_parts.at[me, slot], send_part.at[s], owner_recv_part.at[slot], owner).start()
                remote(stat.at[s], owner_stats.at[me, slot], send_stat.at[s], owner_recv_stat.at[slot], owner).start()

    def leave_all(s):
        here, there = pl.ds(s, STEP), pl.ds(s - shared, STEP)
        t = (s - shared) // STEP
        for d in order:
            to = lax.rem(me + d, devices)
            remote(part.at[here], parts.at[me, there], send_part.at[s], recv_part.at[t], to).start()
            remote(stat.at[here], stats.at[me, there], send_stat.at[s], recv_stat.at[t], to).start()

    neighbour = lax.rem(me + 1, devices)

    def arrived(part_block, stat_block, part_sem, stat_sem):
        remote(part_block, part_block, send_part.at[0], part_sem, neighbour).wait_recv()
        remote(stat_block, stat_block, send_stat.at[0], stat_sem, neighbour).wait_recv()

    most = pl.ds(0, devices - 1)

    def together(parts, stats, slot, s):
        parts[me, slot] = part[s]
        stats[me, slot] = stat[s]
        st = stats[:, slot].reshape(devices, 128)
        scale = jnp.exp2((st - jnp.max(st, 0, keepdims=True)) * factor)
        total = jnp.sum(scale * pltpu.roll(st, 96, 1), 0, keepdims=True)
        scale = scale / total
        out = jnp.zeros((16, 128), jnp.float32)
        for j in range(devices):
            one = scale[j : j + 1]
            even = jnp.sum(jnp.where(lane16 == row16, one, 0.0), 1, keepdims=True)
            odd = jnp.sum(jnp.where(lane16 == row16 + 16, one, 0.0), 1, keepdims=True)
            out = out + parts[j, slot].astype(jnp.float32) * jnp.where(lane16 < 64, even, odd)
        return out

    def write(s, x):
        rows = []
        for j in range(2):
            v = x[8 * j : 8 * (j + 1)]
            w = pltpu.roll(v, 64, 1)
            rows += [jnp.where(upper, v, pltpu.roll(w, 4, 0)), jnp.where(upper, pltpu.roll(v, 4, 0), w)]
        out_ref[s] = jnp.concatenate(rows, 0).astype(jnp.bfloat16)

    def share(s):
        r = slot_of(s)
        arrived(owner_parts.at[most, 0], owner_stats.at[most, 0], owner_recv_part.at[r], owner_recv_stat.at[r])
        done[s] = together(owner_parts, owner_stats, r, s).astype(jnp.bfloat16)
        for d in order:
            remote(done.at[s], done.at[s], send_done.at[r], recv_done.at[jnp.where(s < spread, s // devices, s)], lax.rem(me + d, devices)).start()

    fetch_q.wait()
    for u in range(STEP):
        fetch_k(STEP + u).start()
    for u in range(STEP):
        fetch_k(u).wait()
        score(u, u)
        for t in range(STEP):
            (fetch_k(2 * STEP + t) if u else fetch_v(STEP + t)).start()
    for u in range(STEP):
        fetch_v(u).wait()
    for u in range(STEP):
        attend(u, u)
    for u in range(STEP):
        fetch_v(2 * STEP + u).start()
        fetch_k(3 * STEP + u).start()
    for u in range(STEP):
        fetch_k(STEP + u).wait()
    for u in range(STEP):
        score(STEP + u, STEP + u)
    for u in range(STEP):
        fetch_v(3 * STEP + u).start()
        fetch_k(4 * STEP + u).start()

    steps = sequences // STEP

    def body(i, _):
        s = i * STEP
        now = lax.rem(i, 2) * STEP

        for u in range(STEP):
            fetch_k(s + STEP + u).wait()
            fetch_v(s + u).wait()
        for u in range(STEP):
            score(s + STEP + u, STEP - now + u)
        for u in range(STEP):
            attend(s + u, now + u)
        @pl.when(s + STEP + SLOTS < sequences)
        def _():
            for u in range(STEP):
                fetch_k(s + STEP + SLOTS + u).start()
                fetch_v(s + SLOTS + u).start()

        @pl.when(s + STEP + SLOTS == sequences)
        def _():
            in_pieces(v_hbm, values, v_sem, s + SLOTS)
            for u in range(1, STEP):
                fetch_v(s + SLOTS + u).start()

        @pl.when(i == GREET)
        def _():
            pl.semaphore_wait(barrier, devices - 1)

            def first(t, _):
                leave(t)
                return 0

            lax.fori_loop(0, GREET, first, 0)

        @pl.when(i >= GREET)
        def _():
            leave(i)

        early = devices - 1 - me

        @pl.when(i == 6 + early)
        def _():
            share(me)

        @pl.when((i == 10 + early) & (me >= front))
        def _():
            share(devices + me)

        @pl.when((i == 12 + early // 2) & (me >= front))
        def _():
            share(spread - front + me)

        return 0

    lax.fori_loop(1, steps - 1, body, 0)
    last = sequences - STEP
    for u in range(STEP):
        fetch_v(last + u).wait()
        attend(last + u, last % (2 * STEP) + u)
    leave_all(last)

    def emit_round(r):
        block = done.at[most]
        remote(block, block, send_done.at[0], recv_done.at[r], neighbour).wait_recv()
        for d in range(devices):
            write(r * devices + d, done[r * devices + d].astype(jnp.float32))

    def sent(s, _):
        @pl.when(owner_of(s) != me)
        def _():
            remote(part.at[s], part.at[s], send_part.at[s], recv_part.at[0], neighbour).wait_send()
            remote(stat.at[s], stat.at[s], send_stat.at[s], recv_stat.at[0], neighbour).wait_send()

        return 0

    @pl.when(me < front)
    def _():
        share(devices + me)

    emit_round(0)
    lax.fori_loop(0, shared, sent, 0)

    @pl.when(me < front)
    def _():
        def each(s, _):
            share(s)
            return 0

        lax.fori_loop(first_of(me), jnp.where(me == 0, shared, first_of(me) + STEP), each, 0)

    emit_round(1)

    def come(s, _):
        @pl.when(owner_of(s) != me)
        def _():
            remote(done.at[s], done.at[s], send_done.at[0], recv_done.at[s], neighbour).wait_recv()

        return 0

    lax.fori_loop(spread, shared, come, 0)
    for s in range(spread, shared):
        write(s, done[s].astype(jnp.float32))

    def finish(t, _):
        arrived(parts.at[most, pl.ds(0, STEP)], stats.at[most, pl.ds(0, STEP)], recv_part.at[t], recv_stat.at[t])
        for u in range(STEP):
            write(shared + t * STEP + u, together(parts, stats, t * STEP + u, shared + t * STEP + u))
        return 0

    def sent_all(t, _):
        s = shared + t * STEP
        block = parts.at[most, pl.ds(0, STEP)]
        remote(block, block, send_part.at[s], recv_part.at[0], neighbour).wait_send()
        block = stats.at[most, pl.ds(0, STEP)]
        remote(block, block, send_stat.at[s], recv_stat.at[0], neighbour).wait_send()
        return 0

    lax.fori_loop(0, DIRECT // STEP, sent_all, 0)

    def shared_all(r, _):
        block = done.at[most]
        remote(block, block, send_done.at[r], recv_done.at[0], neighbour).wait_send()
        return 0

    lax.fori_loop(0, jnp.where(me >= front, 3, jnp.where(me == 0, 2 + shared - first_of(0), 2 + STEP)), shared_all, 0)
    finish(DIRECT // STEP - 1, 0)


def solution(mesh):
    devices = mesh.shape["sp"]

    def step(q, k, v):
        n, heads, depth = q.shape
        tokens, groups = k.shape[1:3]
        shared = n - DIRECT
        rounds = 2 + n - DIRECT - (5 * devices // 2 + (devices // 2 - 1) * STEP)
        k, v = (x.transpose(0, 2, 3, 1).reshape(n, groups * depth, tokens) for x in (k, v))
        out = pl.pallas_call(
            functools.partial(kernel, devices),
            out_shape=pltpu.VMEM((n, heads, 128), jnp.bfloat16),
            in_specs=[pl.BlockSpec(memory_space=pl.ANY)] * 3,
            out_specs=pl.BlockSpec(memory_space=pltpu.VMEM),
            scratch_shapes=[
                pltpu.VMEM((n, heads, depth), jnp.bfloat16),
                pltpu.VMEM((SLOTS, groups * depth, tokens), jnp.bfloat16),
                pltpu.VMEM((SLOTS, groups * depth, tokens), jnp.bfloat16),
                pltpu.VMEM((2 * STEP, heads, tokens), jnp.float32),
                pltpu.VMEM((n, 16, 128), jnp.bfloat16),
                pltpu.VMEM((n, 1, 128), jnp.float32),
                pltpu.VMEM((devices, rounds, 16, 128), jnp.bfloat16),
                pltpu.VMEM((devices, rounds, 1, 128), jnp.float32),
                pltpu.VMEM((devices, DIRECT, 16, 128), jnp.bfloat16),
                pltpu.VMEM((devices, DIRECT, 1, 128), jnp.float32),
                pltpu.VMEM((shared, 16, 128), jnp.bfloat16),
                pltpu.SemaphoreType.DMA,
                pltpu.SemaphoreType.DMA((SLOTS,)),
                pltpu.SemaphoreType.DMA((SLOTS,)),
                pltpu.SemaphoreType.DMA((n,)),
                pltpu.SemaphoreType.DMA((n,)),
                pltpu.SemaphoreType.DMA((rounds,)),
                pltpu.SemaphoreType.DMA((rounds,)),
                pltpu.SemaphoreType.DMA((DIRECT // STEP,)),
                pltpu.SemaphoreType.DMA((DIRECT // STEP,)),
                pltpu.SemaphoreType.DMA((rounds,)),
                pltpu.SemaphoreType.DMA((shared,)),
            ],
            compiler_params=pltpu.CompilerParams(collective_id=0, has_side_effects=True, vmem_limit_bytes=60 * 2**20),
        )(q, k, v)
        return out[:, :, :depth]

    return jax.shard_map(
        step,
        mesh=mesh,
        in_specs=(P("dp", None, None), P("dp", "sp", None, None), P("dp", "sp", None, None)),
        out_specs=P("dp", None, None),
        check_vma=False,
    )
```

time: 42.2 us -> 37.5 us (0.89)
  the two profiles are of different devices: /device:TPU:21 before, /device:TPU:52 now
where the time goes in v2:
time: 37.5 us; the launch traced here: 37.4 us
  Pallas kernels  36.7 us (98%)
  local copies, waits for them, and re-layouts  0.71 us (2%)
    pallas_call x1, Pallas kernels, step(): pl.pallas_call(functools.partial(kernel, devices), out_shape=pltpu.VMEM((...  36.7 us

profile of v2, /device:TPU:52, one launch (start us, length us, event | category | flops | bytes accessed | tf_op | source)
XLA Modules:
  0.0 37.4 jit_solution(11099192572006441820)
XLA Ops:
  0.0 36.7 %shard_map.37 = bf16[32,32,128]{2,1,0:T(8,128)(2,1)S(1)} custom-call(bf16[32,32,64]{2,1,0:T(8,128)(2,1)} %q_hbm.1, bf16[32,512,1024]{2,1,0:T(8,128)(2,1)} %bitcast.8, bf16[32,512,1024]{2,1,0:T(8,128)(2,1)} %bitcast.9), custom_call_target="tpu_custom_call" | custom-call | tf_op jit(solution)/shard_map/pallas_call | solution.py:332
  36.7 0.7 %copy.5 = bf16[32,32,64]{2,1,0:T(8,128)(2,1)} copy(bf16[32,32,64]{2,1,0:T(8,128)(2,1)S(1)} %bitcast.7) | data formatting | bytes 262144

commit v3 on v2

--- a/solution.py
+++ b/solution.py
@@ -21,9 +21,9 @@
 ):
     sequences, heads, depth = q_hbm.shape
     shared = sequences - DIRECT
-    spread = 2 * devices
     front = devices // 2
-    near = spread + front
+    spread = shared - (front + 1) * STEP
+    turns = spread // front
     factor = depth**-0.5 * math.log2(math.e)
     me = lax.axis_index("sp")
     order = sorted(range(1, devices), key=lambda d: -min(d, devices - d))
@@ -97,38 +97,30 @@
         both = jnp.where(lane32 == place, jnp.concatenate(highs, 0), 0.0) + jnp.where(lane32 == place + 32, jnp.concatenate(totals, 0), 0.0)
         stat[s] = jnp.sum(both, 0, keepdims=True)
 
-    def owner_of(s):
-        late = jnp.maximum(0, front - 1 - (s - near) // STEP)
-        return jnp.where(s < spread, lax.rem(s, devices), jnp.where(s < near, s - spread + front, late))
-
     def first_of(d):
-        return near + (front - 1 - d) * STEP
-
-    def slot_of(s):
-        return jnp.where(s < spread, s // devices, jnp.where(s < near, 2, 2 + s - first_of(owner_of(s))))
+        return spread + (front - 1 - d) * STEP
 
     def remote(src, dst, send, recv, to):
         return pltpu.make_async_remote_copy(src, dst, send, recv, device(to), pl.DeviceIdType.MESH)
 
     def leave(i):
+        j = i - spread // STEP
         for u in range(STEP):
             s = i * STEP + u
-            owner = jnp.where(i < spread // STEP, lax.rem(i * STEP, devices) + u, jnp.where(i < near // STEP, s - spread + front, jnp.maximum(0, front - 1 + near // STEP - i)))
-            more = jnp.maximum(0, i - (near // STEP + front - 1)) * STEP + u
-            slot = jnp.where(i < spread // STEP, i * STEP // devices, jnp.where(i < near // STEP, 2, 2 + more))
+            owner = jnp.where(j < 0, lax.rem(s, front), jnp.maximum(0, front - 1 - j))
+            slot = jnp.where(j < 0, s // front, turns + u + jnp.maximum(0, j - front + 1) * STEP)
 
             @pl.when(owner != me)
             def _():
-                remote(part.at[s], owner_parts.at[me, slot], send_part.at[s], owner_recv_part.at[slot], owner).start()
-                remote(stat.at[s], owner_stats.at[me, slot], send_stat.at[s], owner_recv_stat.at[slot], owner).start()
+                remote(part.at[s], owner_parts.at[me, slot], send_part.at[0], owner_recv_part.at[slot], owner).start()
+                remote(stat.at[s], owner_stats.at[me, slot], send_stat.at[0], owner_recv_stat.at[slot], owner).start()
 
     def leave_all(s):
         here, there = pl.ds(s, STEP), pl.ds(s - shared, STEP)
-        t = (s - shared) // STEP
         for d in order:
             to = lax.rem(me + d, devices)
-            remote(part.at[here], parts.at[me, there], send_part.at[s], recv_part.at[t], to).start()
-            remote(stat.at[here], stats.at[me, there], send_stat.at[s], recv_stat.at[t], to).start()
+            remote(part.at[here], parts.at[me, there], send_part.at[1], recv_part, to).start()
+            remote(stat.at[here], stats.at[me, there], send_stat.at[1], recv_stat, to).start()
 
     neighbour = lax.rem(me + 1, devices)
 
@@ -161,12 +153,11 @@
             rows += [jnp.where(upper, v, pltpu.roll(w, 4, 0)), jnp.where(upper, pltpu.roll(v, 4, 0), w)]
         out_ref[s] = jnp.concatenate(rows, 0).astype(jnp.bfloat16)
 
-    def share(s):
-        r = slot_of(s)
-        arrived(owner_parts.at[most, 0], owner_stats.at[most, 0], owner_recv_part.at[r], owner_recv_stat.at[r])
-        done[s] = together(owner_parts, owner_stats, r, s).astype(jnp.bfloat16)
+    def share(s, slot, group):
+        arrived(owner_parts.at[most, 0], owner_stats.at[most, 0], owner_recv_part.at[slot], owner_recv_stat.at[slot])
+        done[s] = together(owner_parts, owner_stats, slot, s).astype(jnp.bfloat16)
         for d in order:
-            remote(done.at[s], done.at[s], send_done.at[r], recv_done.at[jnp.where(s < spread, s // devices, s)], lax.rem(me + d, devices)).start()
+            remote(done.at[s], done.at[s], send_done, recv_done.at[group], lax.rem(me + d, devices)).start()
 
     fetch_q.wait()
     for u in range(STEP):
@@ -230,20 +221,6 @@
         def _():
             leave(i)
 
-        early = devices - 1 - me
-
-        @pl.when(i == 6 + early)
-        def _():
-            share(me)
-
-        @pl.when((i == 10 + early) & (me >= front))
-        def _():
-            share(devices + me)
-
-        @pl.when((i == 12 + early // 2) & (me >= front))
-        def _():
-            share(spread - front + me)
-
         return 0
 
     lax.fori_loop(1, steps - 1, body, 0)
@@ -253,71 +230,59 @@
         attend(last + u, last % (2 * STEP) + u)
     leave_all(last)
 
-    def emit_round(r):
-        block = done.at[most]
-        remote(block, block, send_done.at[0], recv_done.at[r], neighbour).wait_recv()
-        for d in range(devices):
-            write(r * devices + d, done[r * devices + d].astype(jnp.float32))
-
-    def sent(s, _):
-        @pl.when(owner_of(s) != me)
-        def _():
-            remote(part.at[s], part.at[s], send_part.at[s], recv_part.at[0], neighbour).wait_send()
-            remote(stat.at[s], stat.at[s], send_stat.at[s], recv_stat.at[0], neighbour).wait_send()
-
-        return 0
-
-    @pl.when(me < front)
+    def await_done(group, count):
+        block = done.at[pl.ds(0, count)]
+        remote(block, block, send_done, recv_done.at[group], neighbour).wait_recv()
+
+    def emit(first, end):
+        for s in range(first, end):
+            write(s, done[s].astype(jnp.float32))
+
+    is_owner, is_first, is_middle = me < front, me == 0, (me > 0) & (me < front)
+
+    @pl.when(is_owner)
     def _():
-        share(devices + me)
-
-    emit_round(0)
-    lax.fori_loop(0, shared, sent, 0)
-
-    @pl.when(me < front)
+        def each(t, _):
+            share(t * front + me, t, 0)
+            return 0
+
+        lax.fori_loop(0, turns, each, 0)
+        for u in range(STEP):
+            share(first_of(me) + u, turns + u, 1)
+
+    def sent(count, own):
+        remote(part.at[pl.ds(0, count)], part.at[pl.ds(0, count)], send_part.at[0], recv_part, neighbour).wait_send()
+        remote(stat.at[pl.ds(0, count)], stat.at[pl.ds(0, count)], send_stat.at[0], recv_stat, neighbour).wait_send()
+        if own:
+            block = owner_parts.at[most, pl.ds(0, own)]
+            remote(block, block, send_done, recv_part, neighbour).wait_send()
+
+    @pl.when(is_first)
     def _():
-        def each(s, _):
-            share(s)
-            return 0
-
-        lax.fori_loop(first_of(me), jnp.where(me == 0, shared, first_of(me) + STEP), each, 0)
-
-    emit_round(1)
-
-    def come(s, _):
-        @pl.when(owner_of(s) != me)
-        def _():
-            remote(done.at[s], done.at[s], send_done.at[0], recv_done.at[s], neighbour).wait_recv()
-
-        return 0
-
-    lax.fori_loop(spread, shared, come, 0)
-    for s in range(spread, shared):
-        write(s, done[s].astype(jnp.float32))
-
-    def finish(t, _):
-        arrived(parts.at[most, pl.ds(0, STEP)], stats.at[most, pl.ds(0, STEP)], recv_part.at[t], recv_stat.at[t])
-        for u in range(STEP):
-            write(shared + t * STEP + u, together(parts, stats, t * STEP + u, shared + t * STEP + u))
-        return 0
-
-    def sent_all(t, _):
-        s = shared + t * STEP
-        block = parts.at[most, pl.ds(0, STEP)]
-        remote(block, block, send_part.at[s], recv_part.at[0], neighbour).wait_send()
-        block = stats.at[most, pl.ds(0, STEP)]
-        remote(block, block, send_stat.at[s], recv_stat.at[0], neighbour).wait_send()
-        return 0
-
-    lax.fori_loop(0, DIRECT // STEP, sent_all, 0)
-
-    def shared_all(r, _):
-        block = done.at[most]
-        remote(block, block, send_done.at[r], recv_done.at[0], neighbour).wait_send()
-        return 0
-
-    lax.fori_loop(0, jnp.where(me >= front, 3, jnp.where(me == 0, 2 + shared - first_of(0), 2 + STEP)), shared_all, 0)
-    finish(DIRECT // STEP - 1, 0)
+        for u in range(STEP, 2 * STEP):
+            share(first_of(0) + u, turns + u, 1)
+        await_done(0, spread - turns)
+        await_done(1, (front - 1) * STEP)
+        sent(shared - turns - 2 * STEP, turns + 2 * STEP)
+
+    @pl.when(is_middle)
+    def _():
+        await_done(0, spread - turns)
+        sent(shared - turns - STEP, turns + STEP)
+        await_done(1, front * STEP)
+
+    @pl.when(jnp.logical_not(is_owner))
+    def _():
+        await_done(0, spread)
+        sent(shared, 0)
+        await_done(1, (front + 1) * STEP)
+
+    emit(0, shared)
+    some_parts, some_stats = parts.at[most, pl.ds(0, STEP)], stats.at[most, pl.ds(0, STEP)]
+    remote(some_parts, some_parts, send_part.at[1], recv_part, neighbour).wait()
+    remote(some_stats, some_stats, send_stat.at[1], recv_stat, neighbour).wait()
+    for u in range(STEP):
+        write(shared + u, together(parts, stats, u, shared + u))
 
 
 def solution(mesh):
@@ -327,7 +292,7 @@
         n, heads, depth = q.shape
         tokens, groups = k.shape[1:3]
         shared = n - DIRECT
-        rounds = 2 + n - DIRECT - (5 * devices // 2 + (devices // 2 - 1) * STEP)
+        own = (shared - (devices // 2 + 1) * STEP) // (devices // 2) + 2 * STEP
         k, v = (x.transpose(0, 2, 3, 1).reshape(n, groups * depth, tokens) for x in (k, v))
         out = pl.pallas_call(
             functools.partial(kernel, devices),
@@ -341,22 +306,22 @@
                 pltpu.VMEM((2 * STEP, heads, tokens), jnp.float32),
                 pltpu.VMEM((n, 16, 128), jnp.bfloat16),
                 pltpu.VMEM((n, 1, 128), jnp.float32),
-                pltpu.VMEM((devices, rounds, 16, 128), jnp.bfloat16),
-                pltpu.VMEM((devices, rounds, 1, 128), jnp.float32),
+                pltpu.VMEM((devices, own, 16, 128), jnp.bfloat16),
+                pltpu.VMEM((devices, own, 1, 128), jnp.float32),
                 pltpu.VMEM((devices, DIRECT, 16, 128), jnp.bfloat16),
                 pltpu.VMEM((devices, DIRECT, 1, 128), jnp.float32),
                 pltpu.VMEM((shared, 16, 128), jnp.bfloat16),
                 pltpu.SemaphoreType.DMA,
                 pltpu.SemaphoreType.DMA((SLOTS,)),
                 pltpu.SemaphoreType.DMA((SLOTS,)),
-                pltpu.SemaphoreType.DMA((n,)),
-                pltpu.SemaphoreType.DMA((n,)),
-                pltpu.SemaphoreType.DMA((rounds,)),
-                pltpu.SemaphoreType.DMA((rounds,)),
-                pltpu.SemaphoreType.DMA((DIRECT // STEP,)),
-                pltpu.SemaphoreType.DMA((DIRECT // STEP,)),
-                pltpu.SemaphoreType.DMA((rounds,)),
-                pltpu.SemaphoreType.DMA((shared,)),
+                pltpu.SemaphoreType.DMA((2,)),
+                pltpu.SemaphoreType.DMA((2,)),
+                pltpu.SemaphoreType.DMA((own,)),
+                pltpu.SemaphoreType.DMA((own,)),
+                pltpu.SemaphoreType.DMA,
+                pltpu.SemaphoreType.DMA,
+                pltpu.SemaphoreType.DMA,
+                pltpu.SemaphoreType.DMA((2,)),
             ],
             compiler_params=pltpu.CompilerParams(collective_id=0, has_side_effects=True, vmem_limit_bytes=60 * 2**20),
         )(q, k, v)

time: 37.5 us -> 35.2 us (0.939)
  the two profiles are of different devices: /device:TPU:52 before, /device:TPU:21 now
where the time goes in v3:
time: 35.2 us
  Pallas kernels  34.4 us (98%)
  local copies, waits for them, and re-layouts  0.71 us (2%)
    pallas_call x1, Pallas kernels, step(): pl.pallas_call(functools.partial(kernel, devices), out_shape=pltpu.VMEM((...  34.4 us
    unnamed x1, local copies, waits for them, and re-layouts  0.71 us

profile of v3, /device:TPU:21, one launch (start us, length us, event | category | flops | bytes accessed | tf_op | source)
XLA Modules:
  0.0 35.2 jit_solution(7066458079153104672)
XLA Ops:
  0.0 34.4 %shard_map.37 = bf16[32,32,128]{2,1,0:T(8,128)(2,1)S(1)} custom-call(bf16[32,32,64]{2,1,0:T(8,128)(2,1)} %q_hbm.1, bf16[32,512,1024]{2,1,0:T(8,128)(2,1)} %bitcast.8, bf16[32,512,1024]{2,1,0:T(8,128)(2,1)} %bitcast.9), custom_call_target="tpu_custom_call" | custom-call | tf_op jit(solution)/shard_map/pallas_call | solution.py:297
  34.4 0.7 %copy.5 = bf16[32,32,64]{2,1,0:T(8,128)(2,1)} copy(bf16[32,32,64]{2,1,0:T(8,128)(2,1)S(1)} %bitcast.7) | data formatting | bytes 262144

commit v4 on v3

--- a/solution.py
+++ b/solution.py
@@ -24,6 +24,7 @@
     front = devices // 2
     spread = shared - (front + 1) * STEP
     turns = spread // front
+    most_own = turns + 2 * STEP
     factor = depth**-0.5 * math.log2(math.e)
     me = lax.axis_index("sp")
     order = sorted(range(1, devices), key=lambda d: -min(d, devices - d))
@@ -103,6 +104,8 @@
     def remote(src, dst, send, recv, to):
         return pltpu.make_async_remote_copy(src, dst, send, recv, device(to), pl.DeviceIdType.MESH)
 
+    neighbour = lax.rem(me + 1, devices)
+
     def leave(i):
         j = i - spread // STEP
         for u in range(STEP):
@@ -110,10 +113,11 @@
             owner = jnp.where(j < 0, lax.rem(s, front), jnp.maximum(0, front - 1 - j))
             slot = jnp.where(j < 0, s // front, turns + u + jnp.maximum(0, j - front + 1) * STEP)
 
-            @pl.when(owner != me)
-            def _():
-                remote(part.at[s], owner_parts.at[me, slot], send_part.at[0], owner_recv_part.at[slot], owner).start()
-                remote(stat.at[s], owner_stats.at[me, slot], send_stat.at[0], owner_recv_stat.at[slot], owner).start()
+            mine = owner == me
+            to, sem = jnp.where(mine, neighbour, owner), jnp.where(mine, most_own, slot)
+            slot = jnp.where(mine, most_own + slot, slot)
+            remote(part.at[s], owner_parts.at[me, slot], send_part.at[0], owner_recv_part.at[sem], to).start()
+            remote(stat.at[s], owner_stats.at[me, slot], send_stat.at[0], owner_recv_stat.at[sem], to).start()
 
     def leave_all(s):
         here, there = pl.ds(s, STEP), pl.ds(s - shared, STEP)
@@ -122,7 +126,6 @@
             remote(part.at[here], parts.at[me, there], send_part.at[1], recv_part, to).start()
             remote(stat.at[here], stats.at[me, there], send_stat.at[1], recv_stat, to).start()
 
-    neighbour = lax.rem(me + 1, devices)
 
     def arrived(part_block, stat_block, part_sem, stat_sem):
         remote(part_block, part_block, send_part.at[0], part_sem, neighbour).wait_recv()
@@ -156,7 +159,7 @@
     def share(s, slot, group):
         arrived(owner_parts.at[most, 0], owner_stats.at[most, 0], owner_recv_part.at[slot], owner_recv_stat.at[slot])
         done[s] = together(owner_parts, owner_stats, slot, s).astype(jnp.bfloat16)
-        for d in order:
+        for d in reversed(order):
             remote(done.at[s], done.at[s], send_done, recv_done.at[group], lax.rem(me + d, devices)).start()
 
     fetch_q.wait()
@@ -184,46 +187,47 @@
 
     steps = sequences // STEP
 
-    def body(i, _):
+    def body(i, leaves, refill):
         s = i * STEP
         now = lax.rem(i, 2) * STEP
-
         for u in range(STEP):
             fetch_k(s + STEP + u).wait()
             fetch_v(s + u).wait()
+        if leaves:
+            leave(i - 1)
         for u in range(STEP):
             score(s + STEP + u, STEP - now + u)
         for u in range(STEP):
             attend(s + u, now + u)
-        @pl.when(s + STEP + SLOTS < sequences)
-        def _():
+        if refill:
             for u in range(STEP):
                 fetch_k(s + STEP + SLOTS + u).start()
                 fetch_v(s + SLOTS + u).start()
 
-        @pl.when(s + STEP + SLOTS == sequences)
-        def _():
-            in_pieces(v_hbm, values, v_sem, s + SLOTS)
+    def early(i, _):
+        body(i, False, True)
+        return 0
+
+    def later(i, _):
+        body(i, True, True)
+        return 0
+
+    def first(i, _):
+        leave(i)
+        return 0
+
+    full = (sequences - SLOTS) // STEP - 1
+    lax.fori_loop(1, GREET, early, 0)
+    pl.semaphore_wait(barrier, devices - 1)
+    lax.fori_loop(0, GREET - 1, first, 0)
+    lax.fori_loop(GREET, full, later, 0)
+    for i in range(full, steps - 1):
+        body(i, True, False)
+        if i == full:
+            in_pieces(v_hbm, values, v_sem, i * STEP + SLOTS)
             for u in range(1, STEP):
-                fetch_v(s + SLOTS + u).start()
-
-        @pl.when(i == GREET)
-        def _():
-            pl.semaphore_wait(barrier, devices - 1)
-
-            def first(t, _):
-                leave(t)
-                return 0
-
-            lax.fori_loop(0, GREET, first, 0)
-
-        @pl.when(i >= GREET)
-        def _():
-            leave(i)
-
-        return 0
-
-    lax.fori_loop(1, steps - 1, body, 0)
+                fetch_v(i * STEP + SLOTS + u).start()
+    leave(steps - 2)
     last = sequences - STEP
     for u in range(STEP):
         fetch_v(last + u).wait()
@@ -250,12 +254,24 @@
         for u in range(STEP):
             share(first_of(me) + u, turns + u, 1)
 
-    def sent(count, own):
-        remote(part.at[pl.ds(0, count)], part.at[pl.ds(0, count)], send_part.at[0], recv_part, neighbour).wait_send()
-        remote(stat.at[pl.ds(0, count)], stat.at[pl.ds(0, count)], send_stat.at[0], recv_stat, neighbour).wait_send()
+    def sent(own):
+        some, few = part.at[pl.ds(0, shared)], stat.at[pl.ds(0, shared)]
+        remote(some, some, send_part.at[0], recv_part, neighbour).wait_send()
+        remote(few, few, send_stat.at[0], recv_stat, neighbour).wait_send()
         if own:
             block = owner_parts.at[most, pl.ds(0, own)]
             remote(block, block, send_done, recv_part, neighbour).wait_send()
+
+    def unread(count):
+        arrived(part.at[pl.ds(0, count)], stat.at[pl.ds(0, count)], owner_recv_part.at[most_own], owner_recv_stat.at[most_own])
+
+    @pl.when(me == 1)
+    def _():
+        unread(most_own)
+
+    @pl.when((me > 1) & (me <= front))
+    def _():
+        unread(turns + STEP)
 
     @pl.when(is_first)
     def _():
@@ -263,18 +279,18 @@
             share(first_of(0) + u, turns + u, 1)
         await_done(0, spread - turns)
         await_done(1, (front - 1) * STEP)
-        sent(shared - turns - 2 * STEP, turns + 2 * STEP)
+        sent(most_own)
 
     @pl.when(is_middle)
     def _():
         await_done(0, spread - turns)
-        sent(shared - turns - STEP, turns + STEP)
+        sent(turns + STEP)
         await_done(1, front * STEP)
 
     @pl.when(jnp.logical_not(is_owner))
     def _():
         await_done(0, spread)
-        sent(shared, 0)
+        sent(0)
         await_done(1, (front + 1) * STEP)
 
     emit(0, shared)
@@ -306,8 +322,8 @@
                 pltpu.VMEM((2 * STEP, heads, tokens), jnp.float32),
                 pltpu.VMEM((n, 16, 128), jnp.bfloat16),
                 pltpu.VMEM((n, 1, 128), jnp.float32),
-                pltpu.VMEM((devices, own, 16, 128), jnp.bfloat16),
-                pltpu.VMEM((devices, own, 1, 128), jnp.float32),
+                pltpu.VMEM((devices, 2 * own, 16, 128), jnp.bfloat16),
+                pltpu.VMEM((devices, 2 * own, 1, 128), jnp.float32),
                 pltpu.VMEM((devices, DIRECT, 16, 128), jnp.bfloat16),
                 pltpu.VMEM((devices, DIRECT, 1, 128), jnp.float32),
                 pltpu.VMEM((shared, 16, 128), jnp.bfloat16),
@@ -316,8 +332,8 @@
                 pltpu.SemaphoreType.DMA((SLOTS,)),
                 pltpu.SemaphoreType.DMA((2,)),
                 pltpu.SemaphoreType.DMA((2,)),
-                pltpu.SemaphoreType.DMA((own,)),
-                pltpu.SemaphoreType.DMA((own,)),
+                pltpu.SemaphoreType.DMA((own + 1,)),
+                pltpu.SemaphoreType.DMA((own + 1,)),
                 pltpu.SemaphoreType.DMA,
                 pltpu.SemaphoreType.DMA,
                 pltpu.SemaphoreType.DMA,

time: 35.2 us -> 34.8 us (0.989)
  Pallas kernels: 34.4 us -> 33.9 us
    pallas_call x1, Pallas kernels: 34.4 us -> 33.9 us  [step(): pl.pallas_call(functools.partial(kernel, devices), out_shape=pltpu.VMEM((...]
where the time goes in v4:
time: 34.8 us; the launch traced here: 34.7 us
  Pallas kernels  33.9 us (97%)
  local copies, waits for them, and re-layouts  0.71 us (2%)
    pallas_call x1, Pallas kernels, step(): pl.pallas_call(functools.partial(kernel, devices), out_shape=pltpu.VMEM((...  33.9 us
    unnamed x1, local copies, waits for them, and re-layouts  0.71 us

profile of v4, /device:TPU:21, one launch (start us, length us, event | category | flops | bytes accessed | tf_op | source)
XLA Modules:
  0.0 34.7 jit_solution(5309705634067640391)
XLA Ops:
  0.0 33.9 %shard_map.37 = bf16[32,32,128]{2,1,0:T(8,128)(2,1)S(1)} custom-call(bf16[32,32,64]{2,1,0:T(8,128)(2,1)} %q_hbm.1, bf16[32,512,1024]{2,1,0:T(8,128)(2,1)} %bitcast.8, bf16[32,512,1024]{2,1,0:T(8,128)(2,1)} %bitcast.9), custom_call_target="tpu_custom_call" | custom-call | tf_op jit(solution)/shard_map/pallas_call | solution.py:313
  34.0 0.7 %copy.5 = bf16[32,32,64]{2,1,0:T(8,128)(2,1)} copy(bf16[32,32,64]{2,1,0:T(8,128)(2,1)S(1)} %bitcast.7) | data formatting | bytes 262144
